TPU v7x, 32 devices: a whole 2x2x4 slice. The times are simulated.
32 devices in a mesh: items: 8 (over z, y), users: 4 (over x, core).
Axes of the slice: x: 2, y: 2, z: 4, core: 2. Of those that a mesh axis runs over, the one named last changes fastest.
Arguments:
- user_emb: bfloat16 [4096, 256], P('users', 'items'), as said below
- item_emb: bfloat16 [262144, 256], P('items'), as said below
- target: int32 [4096], P('users'), may hold values from 0 to 262143
- history: int32 [4096, 32], P('users'), may hold values from 0 to 262143, as said below
Outputs:
- log_rank: float32 [4096], P('users')
- metrics: float32 [2], replicated
Inputs may be any that keep to these rules, and one draw needn't show every extreme that they name: history[u, k] lies in [k * 8192, (k + 1) * 8192); a user's history entries are thus distinct. `item_emb`: rows of norm about one. `user_emb`: entries of order one.
All inputs are finite; a program needn't handle non-finite values.
Results may differ from a plain program's by a relative error of at most 0.0003.
Values may be sent and summed in bfloat16 or wider, within the bound.
A program may use at most 64 MiB of HBM per device.

v0:
```python
import jax
import jax.numpy as jnp
from jax import lax
from jax.sharding import PartitionSpec as P

sharpness = 4.0


def body(user_emb, item_emb, target, history):
    item_dev = item_emb.shape[0]
    shard = lax.axis_index("items")
    start = shard * item_dev
    local_t = target - start
    inside = (local_t >= 0) & (local_t < item_dev)
    own_rows = item_emb[jnp.clip(local_t, 0, item_dev - 1)]
    users = lax.all_gather(user_emb, "items", axis=1, tiled=True)
    partial_t = jnp.sum(users.astype(jnp.float32) * own_rows.astype(jnp.float32), axis=1)
    tscore = lax.psum(jnp.where(inside, partial_t, 0.0), "items")
    n_items = lax.axis_size("items")
    n_users = lax.axis_size("users")
    u_dev = users.shape[0]
    blk = min(item_dev, 4096)
    nblk = item_dev // blk

    def add_block(index, total):
        rows = lax.dynamic_slice_in_dim(item_emb, index * blk, blk, 0)
        score = lax.dot_general(
            users, rows, (((1,), (1,)), ((), ())), preferred_element_type=jnp.float32
        )
        return total + jnp.sum(jax.nn.sigmoid(sharpness * (score - tscore[:, None])), axis=1)

    total = lax.fori_loop(0, nblk, add_block, jnp.zeros((u_dev,), jnp.float32))
    per_shard = history.shape[1] // n_items
    own_hist = lax.dynamic_slice_in_dim(history, shard * per_shard, per_shard, 1)
    hrows = item_emb[own_hist - start]
    hscore = jnp.einsum("ud,uhd->uh", users, hrows, preferred_element_type=jnp.float32)
    local = total - jnp.sum(jax.nn.sigmoid(sharpness * (hscore - tscore[:, None])), axis=1)
    seen = jnp.any(history == target[:, None], axis=1)
    correction = jnp.where(seen, 0.0, 0.5).astype(jnp.float32)
    all_users = u_dev * n_users
    above = lax.psum(local, "items") - correction
    rank = 1.0 + above
    log_rank = jnp.log(rank)
    hit = jax.nn.sigmoid(10.5 - rank)
    gain = hit / jnp.log2(1.0 + rank)
    hit_sum, gain_sum = lax.psum((jnp.sum(hit), jnp.sum(gain)), "users")
    metrics = jnp.stack([hit_sum, gain_sum]) / all_users
    return (log_rank, metrics)


def solution(mesh):
    return jax.shard_map(
        body,
        mesh=mesh,
        in_specs=(P("users", "items"), P("items", None), P("users"), P("users", None)),
        out_specs=(P("users"), P()),
        check_vma=False,
    )
```

profile of v0, /device:TPU:0, one launch (start us, length us, event | category | flops | bytes accessed | tf_op | source)
XLA Modules:
  0.0 174.1 jit_solution(5118468006411309888)
XLA Ops:
  0.6 0.0 copy-start.1
  0.6 0.0 copy-start.2
  0.7 0.8 compare_select_fusion
  1.5 0.2 copy.14
  1.7 0.3 reshape.17
  2.0 20.9 %gather_fusion.1 = bf16[4096,256]{1,0:T(8,128)(2,1)S(1)} fusion(bf16[32768,256]{1,0:T(8,128)(2,1)} %param.7, s32[4096]{0:T(1024)S(1)} %broadcast_clamp_fusion), kind=kCustom, calls=%fused_computation.1 | custom fusion | bytes 4210688 | tf_op jit(solution)/shard_map/gather | solution.py:35
  22.9 2.1 %reshape.16 = bf16[1024,4,256]{2,1,0:T(4,128)(2,1)} reshape(bf16[4096,256]{1,0:T(8,128)(2,1)S(1)} %gather_fusion.1) | data formatting | bytes 4194304 | tf_op jit(solution)/shard_map/gather | solution.py:35
  25.0 0.0 copy-done.1
  25.0 33.0 %all_gather.3 = bf16[1024,256]{0,1:T(8,128)(2,1)S(1)} all-gather(bf16[1024,32]{0,1:T(8,128)(2,1)S(1)} %copy-done.1), channel_id=1, replica_groups=mesh['items'=8,'users'=4] {'items'}, dimensions={1}, use_global_device_ids=true | all-gather | bytes 589824 | tf_op jit(solution)/shard_map/all_gather | solution.py:16
  58.0 0.2 copy.20
  58.2 2.9 %multiply_reduce_fusion = f32[1024,4]{1,0:T(8,128)S(1)} fusion(f32[1024,256]{1,0:T(8,128)S(1)} %copy.20, bf16[1024,4,256]{2,1,0:T(4,128)(2,1)} %reshape.16), kind=kLoop, calls=%fused_computation.7 | loop fusion | flops 3141632 | bytes 3162112
  61.1 0.2 copy.19
  61.3 0.0 copy-done.2
  61.3 11.4 %gather_fusion = bf16[1024,256]{1,0:T(8,128)(2,1)S(1)} fusion(bf16[32768,256]{1,0:T(8,128)(2,1)} %param.7, s32[1024]{0:T(1024)S(1)} %fusion.4), kind=kCustom, calls=%fused_computation | custom fusion | bytes 1052672 | tf_op jit(solution)/shard_map/gather | solution.py:15
  72.7 0.2 copy.13
  73.0 0.2 multiply_reduce_fusion.1
  73.2 21.5 %psum.28 = f32[1024]{0:T(1024)S(1)} all-reduce(f32[1024]{0:T(1024)S(1)} %and_select_fusion), channel_id=1, replica_groups=mesh['items'=8,'users'=4] {'items'}, use_global_device_ids=true, to_apply=%region_1.2 | all-reduce | flops 1024 | bytes 8192 | tf_op jit(solution)/shard_map/psum | solution.py:18
  94.8 0.0 copy-start
  94.8 52.7 %while.14 = (s32[]{:T(128)}, f32[1024]{0:T(1024)S(1)}, bf16[32768,256]{1,0:T(8,128)(2,1)}, bf16[1024,256]{1,0:T(8,128)(2,1)S(1)}, f32[1024]{0:T(1024)S(1)}, /*index=5*/s32[]{:T(128)}, s32[]{:T(128)}, s32[]{:T(128)}, s32[]{:T(128)}) while((s32[]{:T(128)}, f32[1024]{0:T(1024)S(1)}, bf16[32768,256]{1,0:T(8,128)(2,1)}, ...), condition=%wide.region_4.5_spmd.clone, body=%wide.region_2.4_spmd.clone.sunk | while | flops 2172650496 | bytes 2642073 | solution.py:32
  94.8 6.6 %fusion.11 = f32[1024]{0:T(1024)S(1)} fusion(bf16[1024,256]{1,0:T(8,128)(2,1)S(1)} %get-tuple-element.192, f32[1024]{0:T(1024)S(1)} %get-tuple-element.193, bf16[32768,256]{1,0:T(8,128)(2,1)} %get-tuple-element.191, s32[]{:T(128)S(6)} %select_n.43), kind=kOutput, calls=%fused_computation.3.clone.1 | convolution fusion | flops 2172648448 | bytes 2629636 | tf_op jit(solution)/shard_map/while/body/eval_jaxpr/dot_general | solution.py:27
  101.4 6.5 %fusion.11 = f32[1024]{0:T(1024)S(1)} fusion(bf16[1024,256]{1,0:T(8,128)(2,1)S(1)} %get-tuple-element.192, f32[1024]{0:T(1024)S(1)} %get-tuple-element.193, bf16[32768,256]{1,0:T(8,128)(2,1)} %get-tuple-element.191, s32[]{:T(128)S(6)} %select_n.43), kind=kOutput, calls=%fused_computation.3.clone.1 | convolution fusion | flops 2172648448 | bytes 2629636 | tf_op jit(solution)/shard_map/while/body/eval_jaxpr/dot_general | solution.py:27
  108.0 6.5 %fusion.11 = f32[1024]{0:T(1024)S(1)} fusion(bf16[1024,256]{1,0:T(8,128)(2,1)S(1)} %get-tuple-element.192, f32[1024]{0:T(1024)S(1)} %get-tuple-element.193, bf16[32768,256]{1,0:T(8,128)(2,1)} %get-tuple-element.191, s32[]{:T(128)S(6)} %select_n.43), kind=kOutput, calls=%fused_computation.3.clone.1 | convolution fusion | flops 2172648448 | bytes 2629636 | tf_op jit(solution)/shard_map/while/body/eval_jaxpr/dot_general | solution.py:27
  114.6 6.5 %fusion.11 = f32[1024]{0:T(1024)S(1)} fusion(bf16[1024,256]{1,0:T(8,128)(2,1)S(1)} %get-tuple-element.192, f32[1024]{0:T(1024)S(1)} %get-tuple-element.193, bf16[32768,256]{1,0:T(8,128)(2,1)} %get-tuple-element.191, s32[]{:T(128)S(6)} %select_n.43), kind=kOutput, calls=%fused_computation.3.clone.1 | convolution fusion | flops 2172648448 | bytes 2629636 | tf_op jit(solution)/shard_map/while/body/eval_jaxpr/dot_general | solution.py:27
  121.2 6.5 %fusion.11 = f32[1024]{0:T(1024)S(1)} fusion(bf16[1024,256]{1,0:T(8,128)(2,1)S(1)} %get-tuple-element.192, f32[1024]{0:T(1024)S(1)} %get-tuple-element.193, bf16[32768,256]{1,0:T(8,128)(2,1)} %get-tuple-element.191, s32[]{:T(128)S(6)} %select_n.43), kind=kOutput, calls=%fused_computation.3.clone.1 | convolution fusion | flops 2172648448 | bytes 2629636 | tf_op jit(solution)/shard_map/while/body/eval_jaxpr/dot_general | solution.py:27
  127.8 6.5 %fusion.11 = f32[1024]{0:T(1024)S(1)} fusion(bf16[1024,256]{1,0:T(8,128)(2,1)S(1)} %get-tuple-element.192, f32[1024]{0:T(1024)S(1)} %get-tuple-element.193, bf16[32768,256]{1,0:T(8,128)(2,1)} %get-tuple-element.191, s32[]{:T(128)S(6)} %select_n.43), kind=kOutput, calls=%fused_computation.3.clone.1 | convolution fusion | flops 2172648448 | bytes 2629636 | tf_op jit(solution)/shard_map/while/body/eval_jaxpr/dot_general | solution.py:27
  134.4 6.5 %fusion.11 = f32[1024]{0:T(1024)S(1)} fusion(bf16[1024,256]{1,0:T(8,128)(2,1)S(1)} %get-tuple-element.192, f32[1024]{0:T(1024)S(1)} %get-tuple-element.193, bf16[32768,256]{1,0:T(8,128)(2,1)} %get-tuple-element.191, s32[]{:T(128)S(6)} %select_n.43), kind=kOutput, calls=%fused_computation.3.clone.1 | convolution fusion | flops 2172648448 | bytes 2629636 | tf_op jit(solution)/shard_map/while/body/eval_jaxpr/dot_general | solution.py:27
  140.9 6.5 %fusion.11 = f32[1024]{0:T(1024)S(1)} fusion(bf16[1024,256]{1,0:T(8,128)(2,1)S(1)} %get-tuple-element.192, f32[1024]{0:T(1024)S(1)} %get-tuple-element.193, bf16[32768,256]{1,0:T(8,128)(2,1)} %get-tuple-element.191, s32[]{:T(128)S(6)} %select_n.43), kind=kOutput, calls=%fused_computation.3.clone.1 | convolution fusion | flops 2172648448 | bytes 2629636 | tf_op jit(solution)/shard_map/while/body/eval_jaxpr/dot_general | solution.py:27
  147.5 17.1 %psum.29 = f32[1024]{0:T(1024)S(1)} all-reduce(f32[1024]{0:T(1024)S(1)} %sub.59), channel_id=1, replica_groups=mesh['items'=8,'users'=4] {'items'}, use_global_device_ids=true, to_apply=%region_6.7 | all-reduce | flops 1024 | bytes 8192 | tf_op jit(solution)/shard_map/psum | solution.py:41
  164.7 0.0 copy-done
  164.7 1.3 divide_reduce_fusion.1
  166.0 6.3 %all-reduce = (f32[1]{0:T(128)}, f32[1]{0:T(128)}) all-reduce(f32[1]{0:T(128)} %bitcast.2, f32[1]{0:T(128)} %bitcast.1), channel_id=1, replica_groups=mesh['items'=8,'users'=4] {'users'}, use_global_device_ids=true, to_apply=%region_11.12 | all-reduce | flops 2 | bytes 16 | tf_op jit(solution)/shard_map/psum | solution.py:46
  172.3 1.8 %maximum_multiply_fusion = f32[2]{0:T(128)} fusion(f32[1]{0:T(128)} %get-tuple-element.137, f32[1]{0:T(128)} %get-tuple-element.138), kind=kLoop, calls=%fused_computation.22 | loop fusion | flops 4 | bytes 16 | tf_op jit(solution)/shard_map/div | solution.py:47
  (15 shorter events, 0.1 us)
Async XLA Ops:
  0.6 24.4 %copy-start.1 = (bf16[1024,32]{0,1:T(8,128)(2,1)S(1)}, bf16[1024,32]{0,1:T(8,128)(2,1)}, u32[]{:S(2)}) copy-start(bf16[1024,32]{0,1:T(8,128)(2,1)} %param.6) | copy-start | bytes 196612
  0.6 60.7 %copy-start.2 = (s32[1024]{0:T(1024)S(1)}, s32[1024]{0:T(1024)}, u32[]{:S(2)}) copy-start(s32[1024]{0:T(1024)} %param.8) | copy-start | bytes 12292
  94.8 69.9 %copy-start = (s32[1024,32]{0,1:T(8,128)S(1)}, s32[1024,32]{0,1:T(8,128)}, u32[]{:S(2)}) copy-start(s32[1024,32]{0,1:T(8,128)} %param.9) | copy-start | bytes 393220
where the time goes:
time: 175 us; the launch traced here: 174 us
  blocking collectives  78 us (45%)
  matrix products  52.3 us (30%)
  local copies, waits for them, and re-layouts  35.5 us (20%)
  other arithmetic  7.14 us (4%)
    dot_general x8, matrix products, add_block(): lax.dot_general(users, rows, (((1,), (1,)), ((), ())), preferred_element_...  52.3 us
    all_gather x1, blocking collectives, body(): users = lax.all_gather(user_emb, 'items', axis=1, tiled=True)  33 us
    gather x2, local copies, waits for them, and re-layouts, body(): hrows = item_emb[own_hist - start]  23 us
    psum x1, blocking collectives, body(): tscore = lax.psum(jnp.where(inside, partial_t, 0.0), 'items')  21.5 us
    psum x1, blocking collectives, body(): above = lax.psum(local, 'items') - correction  17.1 us
    gather x1, local copies, waits for them, and re-layouts, body(): own_rows = item_emb[jnp.clip(local_t, 0, item_dev - 1)]  11.4 us
    psum x1, blocking collectives, body(): hit_sum, gain_sum = lax.psum((jnp.sum(hit), jnp.sum(gain)), 'users')  6.3 us

commit v1 on v0

v1 whole, which is shorter than its diff:
```python
import functools

import jax
import jax.numpy as jnp
from jax import lax
from jax.experimental import pallas as pl
from jax.experimental.pallas import tpu as pltpu
from jax.sharding import PartitionSpec as P

MESH = pl.DeviceIdType.MESH
CHUNK = 2048
GROUPS = 64
LOG_GROUPS = 6
SLOTS = 4
WIDTH = 512


def exchange(axis, n, me, src, dst, send, recv):
    copies = []
    for off in range(1, n):
        peer = lax.rem(me + off, n)
        copies.append(
            pltpu.make_async_remote_copy(
                src_ref=src,
                dst_ref=dst,
                send_sem=send.at[off - 1],
                recv_sem=recv.at[off - 1],
                device_id={axis: peer},
                device_id_type=MESH,
            )
        )
    for c in copies:
        c.start()
    return copies


def kernel(
    n, m, u_ref, own_ref, item_ref, tgt_ref, hist_ref, log_ref, met_ref,
    gath, w, buf, tpart, tslots, apart, aslots, mpart, mslots, tvec, acc,
    sem_item, sem_u, us, ur, ts, tr, as_, ar, ms, mr,
):
    me = lax.axis_index("items")
    grp = lax.axis_index("users")
    dsh, u_dev = u_ref.shape
    item_dev = item_ref.shape[0]
    n_chunks = item_dev // CHUNK
    per_shard = hist_ref.shape[0] // n
    span = item_dev // per_shard

    def fetch(i):
        return pltpu.make_async_copy(
            item_ref.at[pl.ds(i * CHUNK, CHUNK), :], buf.at[lax.rem(i, SLOTS)], sem_item.at[lax.rem(i, SLOTS)]
        )

    for i in range(min(SLOTS - 1, n_chunks)):
        fetch(i).start()
    mine = pl.ds(pl.multiple_of(me * dsh, dsh), dsh)
    keep = pltpu.make_async_copy(u_ref, gath.at[mine, :], sem_u)
    keep.start()

    barrier = pltpu.get_barrier_semaphore()
    for off in range(1, n):
        pl.semaphore_signal(barrier, inc=1, device_id={"items": lax.rem(me + off, n)}, device_id_type=MESH)
    for off in range(1, m):
        pl.semaphore_signal(barrier, inc=1, device_id={"users": lax.rem(grp + off, m)}, device_id_type=MESH)
    pl.semaphore_wait(barrier, n - 1 + m - 1)

    copies = exchange("items", n, me, u_ref, gath.at[mine, :], us, ur)
    keep.wait()
    for c in copies:
        c.wait()
    w[...] = gath[...] * jnp.bfloat16(2)

    step = 256
    eye = lax.broadcasted_iota(jnp.int32, (step, step), 0) == lax.broadcasted_iota(jnp.int32, (step, step), 1)
    for b in range(u_dev // step):
        cols = slice(b * step, (b + 1) * step)
        p = jnp.dot(own_ref[cols, :], w[:, cols], preferred_element_type=jnp.float32)
        p = jnp.sum(jnp.where(eye, p, 0.0), axis=0, keepdims=True)
        local = tgt_ref[:, cols] - me * item_dev
        inside = (local >= 0) & (local < item_dev)
        tpart[:, cols] = jnp.where(inside, p, 0.0)
    tslots[me] = tpart[...]
    copies = exchange("items", n, me, tpart, tslots.at[me], ts, tr)
    for c in copies:
        c.wait()
    tsum = tslots[0]
    for i in range(1, n):
        tsum = tsum + tslots[i]
    tvec[...] = jnp.broadcast_to(tsum, tvec.shape)
    acc[...] = jnp.zeros_like(acc)

    rows = GROUPS * 8
    iota8 = lax.broadcasted_iota(jnp.int32, (8, WIDTH), 0)

    def chunk(i, carry):
        fetch(i).wait()

        @pl.when(i + SLOTS - 1 < n_chunks)
        def _():
            fetch(i + SLOTS - 1).start()

        slot = lax.rem(i, SLOTS)
        k = lax.div(i * CHUNK, span)
        base = i * CHUNK - k * span
        row = me * per_shard + k
        for c in range(u_dev // WIDTH):
            cols = slice(c * WIDTH, (c + 1) * WIDTH)
            h = jnp.broadcast_to(hist_ref[pl.ds(row, 1), cols] - row * span, (8, WIDTH))
            t = tvec[:, cols]
            bits = [(h & (8 << b)) != 0 for b in range(LOG_GROUPS)]
            place = ((h >> (3 + LOG_GROUPS)) << 3) | (h & 7)
            total = acc[:, cols]
            for s in range(CHUNK // rows):
                part = jnp.dot(
                    buf[slot, pl.ds(s * rows, rows), :], w[:, cols], preferred_element_type=jnp.float32
                )
                sums, picks = [], []
                for g in range(GROUPS):
                    tau = jnp.tanh(part[8 * g : 8 * g + 8] - t)
                    lvl, v = 0, tau
                    while sums and sums[-1][0] == lvl:
                        v = sums.pop()[1] + v
                        lvl += 1
                    if lvl == 2:
                        total = total + (v + 4.0)
                    else:
                        sums.append((lvl, v))
                    lvl, v = 0, tau
                    while picks and picks[-1][0] == lvl:
                        v = jnp.where(bits[lvl], v, picks.pop()[1])
                        lvl += 1
                    picks.append((lvl, v))
                tile = lax.div(base, rows) + s
                match = place == iota8 + tile * 8
                total = total - jnp.where(match, picks[0][1] + 1.0, 0.0)
            acc[:, cols] = total
        return carry

    lax.fori_loop(0, n_chunks, chunk, 0)

    apart[...] = 0.5 * jnp.sum(acc[...], axis=0, keepdims=True)
    aslots[me] = apart[...]
    copies = exchange("items", n, me, apart, aslots.at[me], as_, ar)
    seen = jnp.max(jnp.where(hist_ref[...] == tgt_ref[...], 1.0, 0.0), axis=0, keepdims=True)
    for c in copies:
        c.wait()
    total = aslots[0]
    for i in range(1, n):
        total = total + aslots[i]
    rank = 1.0 + (total - jnp.where(seen > 0.5, 0.0, 0.5))
    log_ref[...] = jnp.log(rank)
    hit = jax.nn.sigmoid(10.5 - rank)
    gain = hit / jnp.log2(1.0 + rank)
    hs, gs = hit[:, :128], gain[:, :128]
    for b in range(1, u_dev // 128):
        hs = hs + hit[:, b * 128 : (b + 1) * 128]
        gs = gs + gain[:, b * 128 : (b + 1) * 128]
    mpart[:, :128] = hs
    mpart[:, 128:] = gs
    mslots[grp] = mpart[...]
    copies = exchange("users", m, grp, mpart, mslots.at[grp], ms, mr)
    for c in copies:
        c.wait()
    tot = mslots[0]
    for i in range(1, m):
        tot = tot + mslots[i]
    scale = 1.0 / (u_dev * m)
    met_ref[0] = jnp.sum(tot[:, :128]) * scale
    met_ref[1] = jnp.sum(tot[:, 128:]) * scale


def solution(mesh):
    n, m = mesh.shape["items"], mesh.shape["users"]

    def body(user_emb, item_emb, target, history):
        u_dev, dsh = user_emb.shape
        item_dev, d = item_emb.shape
        own = item_emb[jnp.remainder(target, item_dev)]
        vmem = pl.BlockSpec(memory_space=pltpu.VMEM)
        dma = pltpu.SemaphoreType.DMA
        log_rank, metrics = pl.pallas_call(
            functools.partial(kernel, n, m),
            out_shape=(
                jax.ShapeDtypeStruct((1, u_dev), jnp.float32),
                jax.ShapeDtypeStruct((2,), jnp.float32),
            ),
            in_specs=[vmem, vmem, pl.BlockSpec(memory_space=pl.ANY), vmem, vmem],
            out_specs=(vmem, pl.BlockSpec(memory_space=pltpu.SMEM)),
            scratch_shapes=[
                pltpu.VMEM((d, u_dev), jnp.bfloat16),
                pltpu.VMEM((d, u_dev), jnp.bfloat16),
                pltpu.VMEM((SLOTS, CHUNK, d), jnp.bfloat16),
                pltpu.VMEM((1, u_dev), jnp.float32),
                pltpu.VMEM((n, 1, u_dev), jnp.float32),
                pltpu.VMEM((1, u_dev), jnp.float32),
                pltpu.VMEM((n, 1, u_dev), jnp.float32),
                pltpu.VMEM((1, 256), jnp.float32),
                pltpu.VMEM((m, 1, 256), jnp.float32),
                pltpu.VMEM((8, u_dev), jnp.float32),
                pltpu.VMEM((8, u_dev), jnp.float32),
                dma((SLOTS,)),
                dma(()),
                dma((n - 1,)), dma((n - 1,)),
                dma((n - 1,)), dma((n - 1,)),
                dma((n - 1,)), dma((n - 1,)),
                dma((m - 1,)), dma((m - 1,)),
            ],
            compiler_params=pltpu.CompilerParams(
                collective_id=0, has_side_effects=True, vmem_limit_bytes=48 * 1024 * 1024
            ),
        )(user_emb.T, own, item_emb, target.reshape(1, u_dev), history.T)
        return log_rank.reshape(u_dev), metrics

    return jax.shard_map(
        body,
        mesh=mesh,
        in_specs=(P("users", "items"), P("items", None), P("users"), P("users", None)),
        out_specs=(P("users"), P()),
        check_vma=False,
    )
```

time: 175 us -> 73.5 us (0.42)
  blocking collectives: 78 us -> 0 us
  Pallas kernels: 0 us -> 57 us
  matrix products: 52.3 us -> 0 us
  local copies, waits for them, and re-layouts: 35.5 us -> 14.9 us
  other arithmetic: 7.14 us -> 0.7 us
    pallas_call x0 -> x1, Pallas kernels: none -> 57 us  [body(): pl.pallas_call(functools.partial(kernel, n, m), out_shape=(jax.ShapeDtype...]
    dot_general x8 -> x0, matrix products: 52.3 us -> none  [add_block(): lax.dot_general(users, rows, (((1,), (1,)), ((), ())), preferred_element_...]
    psum x3 -> x0, blocking collectives: 45 us -> none  [the longest x1 21.5 us: body(): tscore = lax.psum(jnp.where(inside, partial_t, 0.0), 'items')]
    all_gather x1 -> x0, blocking collectives: 33 us -> none  [body(): users = lax.all_gather(user_emb, 'items', axis=1, tiled=True)]
    gather x3 -> x1, local copies, waits for them, and re-layouts: 34.4 us -> 11.4 us  [body(): own = item_emb[jnp.remainder(target, item_dev)]]
    unnamed x8, local copies, waits for them, and re-layouts: 0.42 us -> 3.53 us
    unnamed x2 -> x0, other arithmetic: 2.91 us -> none
    div x1 -> x0, other arithmetic: 1.78 us -> none  [body(): metrics = jnp.stack([hit_sum, gain_sum]) / all_users]
where the time goes in v1:
time: 73.5 us; the launch traced here: 73.2 us
  Pallas kernels  57 us (78%)
  local copies, waits for them, and re-layouts  14.9 us (20%)
    pallas_call x1, Pallas kernels, body(): pl.pallas_call(functools.partial(kernel, n, m), out_shape=(jax.ShapeDtype...  57 us
    gather x1, local copies, waits for them, and re-layouts, body(): own = item_emb[jnp.remainder(target, item_dev)]  11.4 us
    unnamed x8, local copies, waits for them, and re-layouts  3.53 us

profile of v1, /device:TPU:0, one launch (start us, length us, event | category | flops | bytes accessed | tf_op | source)
XLA Modules:
  0.0 73.2 jit_solution(8583742522325712905)
XLA Ops:
  0.6 0.7 fusion.1
  1.3 11.4 %gather_fusion = bf16[1024,256]{1,0:T(8,128)(2,1)S(1)} fusion(bf16[32768,256]{1,0:T(8,128)(2,1)} %item_ref.1, s32[1024]{0:T(1024)S(1)} %fusion.1), kind=kCustom, calls=%fused_computation | custom fusion | bytes 1052672 | tf_op jit(solution)/shard_map/gather | solution.py:179
  12.7 0.0 copy-start
  12.7 0.9 %copy-done = s32[1024,32]{0,1:T(8,128)S(1)} copy-done((s32[1024,32]{0,1:T(8,128)S(1)}, s32[1024,32]{0,1:T(8,128)}, u32[]{:S(2)}) %copy-start) | copy-done | bytes 131096
  13.6 0.0 copy-start.1
  13.6 0.8 %copy-done.1 = bf16[1024,32]{0,1:T(8,128)(2,1)S(1)} copy-done((bf16[1024,32]{0,1:T(8,128)(2,1)S(1)}, bf16[1024,32]{0,1:T(8,128)(2,1)}, u32[]{:S(2)}) %copy-start.1) | copy-done | bytes 65560
  14.5 0.0 copy-start.2
  14.5 0.7 copy-done.2
  15.2 57.0 %shard_map.59 = (f32[1,1024]{1,0:T(1,128)S(1)}, f32[2]{0:T(128)S(1)}) custom-call(bf16[32,1024]{1,0:T(8,128)(2,1)S(1)} %bitcast.5, bf16[1024,256]{1,0:T(8,128)(2,1)S(1)} %gather_fusion, bf16[32768,256]{1,0:T(8,128)(2,1)} %item_ref.1, s32[1,1024]{1,0:T(1,128)S(1)} %bitcast.6, s32[32,1024]{1,0:T(8,128)S(1)} %bitcast.4), custom_call_target="tpu_custom_call" | custom-call | tf_op jit(solution)/shard_map/pallas_call | solution.py:182
  72.1 0.6 copy.8
  72.7 0.5 copy.9
Async XLA Ops:
  12.7 0.9 %copy-start = (s32[1024,32]{0,1:T(8,128)S(1)}, s32[1024,32]{0,1:T(8,128)}, u32[]{:S(2)}) copy-start(s32[1024,32]{0,1:T(8,128)} %param.7) | copy-start | bytes 393220
  13.6 0.8 %copy-start.1 = (bf16[1024,32]{0,1:T(8,128)(2,1)S(1)}, bf16[1024,32]{0,1:T(8,128)(2,1)}, u32[]{:S(2)}) copy-start(bf16[1024,32]{0,1:T(8,128)(2,1)} %param.4) | copy-start | bytes 196612
  14.5 0.7 copy-start.2

commit v2 on v1

v2 whole, which is shorter than its diff:
```python
import functools

import jax
import jax.numpy as jnp
from jax import lax
from jax.experimental import pallas as pl
from jax.experimental.pallas import tpu as pltpu
from jax.sharding import PartitionSpec as P

MESH = pl.DeviceIdType.MESH
CHUNK = 4096
GROUPS = 64
LOG_GROUPS = 6
WIDTH = 512
DOT = 512
PARTS = 2
PIECES = 8


def exchange(axis, n, me, src, dst, send, recv):
    copies = []
    for off in range(1, n):
        peer = lax.rem(me + off, n)
        copies.append(
            pltpu.make_async_remote_copy(
                src_ref=src,
                dst_ref=dst,
                send_sem=send.at[off - 1],
                recv_sem=recv.at[off - 1],
                device_id={axis: peer},
                device_id_type=MESH,
            )
        )
    for c in copies:
        c.start()
    return copies


def pick(tgt_ref, item_ref, own_ref, sem):
    item_dev = item_ref.shape[0]
    batch = 16

    def body(i, carry):
        for j in range(batch):
            user = i * batch + j
            local = lax.rem(tgt_ref[user], item_dev)
            row = pl.multiple_of((local >> 3) << 3, 8)
            pltpu.make_async_copy(
                item_ref.at[pl.ds(row, 8), :], own_ref.at[pl.ds(pl.multiple_of(user * 8, 8), 8), :], sem
            ).start()
        return carry

    u_dev = tgt_ref.shape[0]
    lax.fori_loop(0, u_dev // batch, body, 0)
    pltpu.make_async_copy(item_ref.at[pl.ds(0, u_dev * 8), :], own_ref, sem).wait()


def kernel(
    n, m, u_ref, own_ref, item_ref, tgt_ref, hist_ref, log_ref, met_ref,
    gath, w, items, own, tpart, tslots, apart, aslots, mpart, mslots, acc,
    sem_item, sem_own, sem_u, us, ur, ts, tr, as_, ar, ms, mr,
):
    me = lax.axis_index("items")
    grp = lax.axis_index("users")
    dsh, u_dev = u_ref.shape
    item_dev = item_ref.shape[0]
    per_shard = hist_ref.shape[0] // n
    span = item_dev // per_shard
    half = u_dev // PARTS
    piece = item_dev // PIECES

    fetches = []
    for i in range(PIECES):
        part = pl.ds(i * piece, piece)
        fetches.append(pltpu.make_async_copy(item_ref.at[part, :], items.at[part, :], sem_item.at[i]))
    mine = pl.ds(pl.multiple_of(me * dsh, dsh), dsh)
    keep = pltpu.make_async_copy(u_ref, gath.at[mine, :], sem_u)
    keep.start()
    tiles = pltpu.make_async_copy(own_ref, own, sem_own)
    tiles.start()
    for f in fetches:
        f.start()

    barrier = pltpu.get_barrier_semaphore()
    for off in range(1, n):
        pl.semaphore_signal(barrier, inc=1, device_id={"items": lax.rem(me + off, n)}, device_id_type=MESH)
    for off in range(1, m):
        pl.semaphore_signal(barrier, inc=1, device_id={"users": lax.rem(grp + off, m)}, device_id_type=MESH)
    pl.semaphore_wait(barrier, n - 1 + m - 1)

    ucopies = []
    for p in range(PARTS):
        cols = slice(p * half, (p + 1) * half)
        ucopies.append(exchange("items", n, me, u_ref.at[:, cols], gath.at[mine, cols], us.at[p], ur.at[p]))
    acc[...] = jnp.zeros_like(acc)
    keep.wait()
    tiles.wait()
    lane = lax.broadcasted_iota(jnp.int32, (8, 128), 1)
    sub = lax.broadcasted_iota(jnp.int32, (8, 128), 0)
    tcopies = []
    for p in range(PARTS):
        for c in ucopies[p]:
            c.wait()
        cols = slice(p * half, (p + 1) * half)
        w[:, cols] = gath[:, cols] * jnp.bfloat16(2)
        for b in range(half // 128):
            at = p * half + b * 128
            pc = jnp.dot(own[at * 8 : at * 8 + 1024, :], w[:, at : at + 128], preferred_element_type=jnp.float32)
            got = pc[:8]
            for r in range(1, 128):
                got = jnp.where(lane == r, pc[8 * r : 8 * r + 8], got)
            tgt = tgt_ref[:, at : at + 128]
            got = jnp.sum(jnp.where(sub == (tgt & 7), got, 0.0), axis=0, keepdims=True)
            local = tgt - me * item_dev
            tpart[p, :, b * 128 : (b + 1) * 128] = jnp.where((local >= 0) & (local < item_dev), got, 0.0)
        tslots[p, me] = tpart[p]
        tcopies.append(exchange("items", n, me, tpart.at[p], tslots.at[p, me], ts.at[p], tr.at[p]))

    rows = GROUPS * 8
    for f in fetches:
        f.wait()
    iota8 = lax.broadcasted_iota(jnp.int32, (8, WIDTH), 0)
    acopies = []
    for p in range(PARTS):
        for c in tcopies[p]:
            c.wait()
        tsum = tslots[p, 0]
        for i in range(1, n):
            tsum = tsum + tslots[p, i]
        tpart[p] = tsum

        def chunk(i, carry, p=p):
            k = lax.div(i * CHUNK, span)
            base = i * CHUNK - k * span
            row = me * per_shard + k
            for c in range(half // WIDTH):
                lo = p * half + c * WIDTH
                cols = slice(lo, lo + WIDTH)
                h = jnp.broadcast_to(hist_ref[pl.ds(row, 1), cols] - row * span, (8, WIDTH))
                t = jnp.broadcast_to(tpart[p, :, c * WIDTH : (c + 1) * WIDTH], (8, WIDTH))
                bits = [(h & (8 << b)) != 0 for b in range(LOG_GROUPS)]
                place = ((h >> (3 + LOG_GROUPS)) << 3) | (h & 7)
                total = acc[:, cols]
                for s in range(CHUNK // rows):
                    sums, picks = [], []
                    for q in range(rows // DOT):
                        at = pl.multiple_of(i * CHUNK + s * rows + q * DOT, DOT)
                        part = jnp.dot(items[pl.ds(at, DOT), :], w[:, cols], preferred_element_type=jnp.float32)
                        for g in range(DOT // 8):
                            tau = jnp.tanh(part[8 * g : 8 * g + 8] - t)
                            lvl, v = 0, tau
                            while sums and sums[-1][0] == lvl:
                                v = sums.pop()[1] + v
                                lvl += 1
                            if lvl == 2:
                                total = total + (v + 4.0)
                            else:
                                sums.append((lvl, v))
                            lvl, v = 0, tau
                            while picks and picks[-1][0] == lvl:
                                v = jnp.where(bits[lvl], v, picks.pop()[1])
                                lvl += 1
                            picks.append((lvl, v))
                    tile = lax.div(base, rows) + s
                    match = place == iota8 + tile * 8
                    total = total - jnp.where(match, picks[0][1] + 1.0, 0.0)
                acc[:, cols] = total
            return carry

        lax.fori_loop(0, item_dev // CHUNK, chunk, 0)
        cols = slice(p * half, (p + 1) * half)
        apart[p] = 0.5 * jnp.sum(acc[:, cols], axis=0, keepdims=True)
        aslots[p, me] = apart[p]
        acopies.append(exchange("items", n, me, apart.at[p], aslots.at[p, me], as_.at[p], ar.at[p]))

    seen = jnp.max(jnp.where(hist_ref[...] == tgt_ref[...], 1.0, 0.0), axis=0, keepdims=True)
    hs = jnp.zeros((1, 128), jnp.float32)
    gs = jnp.zeros((1, 128), jnp.float32)
    for p in range(PARTS):
        cols = slice(p * half, (p + 1) * half)
        for c in acopies[p]:
            c.wait()
        total = aslots[p, 0]
        for i in range(1, n):
            total = total + aslots[p, i]
        rank = 1.0 + (total - jnp.where(seen[:, cols] > 0.5, 0.0, 0.5))
        log_ref[:, cols] = jnp.log(rank)
        hit = jax.nn.sigmoid(10.5 - rank)
        gain = hit / jnp.log2(1.0 + rank)
        for b in range(half // 128):
            hs = hs + hit[:, b * 128 : (b + 1) * 128]
            gs = gs + gain[:, b * 128 : (b + 1) * 128]
    mpart[:, :128] = hs
    mpart[:, 128:] = gs
    mslots[grp] = mpart[...]
    copies = exchange("users", m, grp, mpart, mslots.at[grp], ms, mr)
    for c in copies:
        c.wait()
    tot = mslots[0]
    for i in range(1, m):
        tot = tot + mslots[i]
    scale = 1.0 / (u_dev * m)
    met_ref[0] = jnp.sum(tot[:, :128]) * scale
    met_ref[1] = jnp.sum(tot[:, 128:]) * scale


def solution(mesh):
    n, m = mesh.shape["items"], mesh.shape["users"]

    def body(user_emb, item_emb, target, history):
        u_dev, dsh = user_emb.shape
        item_dev, d = item_emb.shape
        half = u_dev // PARTS
        vmem = pl.BlockSpec(memory_space=pltpu.VMEM)
        hbm = pl.BlockSpec(memory_space=pltpu.HBM)
        dma = pltpu.SemaphoreType.DMA
        own = pl.pallas_call(
            pick,
            out_shape=jax.ShapeDtypeStruct((u_dev * 8, d), jnp.bfloat16),
            in_specs=[pl.BlockSpec(memory_space=pltpu.SMEM), pl.BlockSpec(memory_space=pltpu.HBM)],
            out_specs=vmem,
            scratch_shapes=[dma(())],
        )(target, item_emb)
        log_rank, metrics = pl.pallas_call(
            functools.partial(kernel, n, m),
            out_shape=(
                jax.ShapeDtypeStruct((1, u_dev), jnp.float32),
                jax.ShapeDtypeStruct((2,), jnp.float32),
            ),
            in_specs=[vmem, hbm, hbm, vmem, vmem],
            out_specs=(vmem, pl.BlockSpec(memory_space=pltpu.SMEM)),
            scratch_shapes=[
                pltpu.VMEM((d, u_dev), jnp.bfloat16),
                pltpu.VMEM((d, u_dev), jnp.bfloat16),
                pltpu.VMEM((item_dev, d), jnp.bfloat16),
                pltpu.VMEM((u_dev * 8, d), jnp.bfloat16),
                pltpu.VMEM((PARTS, 1, half), jnp.float32),
                pltpu.VMEM((PARTS, n, 1, half), jnp.float32),
                pltpu.VMEM((PARTS, 1, half), jnp.float32),
                pltpu.VMEM((PARTS, n, 1, half), jnp.float32),
                pltpu.VMEM((1, 256), jnp.float32),
                pltpu.VMEM((m, 1, 256), jnp.float32),
                pltpu.VMEM((8, u_dev), jnp.float32),
                dma((PIECES,)),
                dma(()),
                dma(()),
                dma((PARTS, n - 1)), dma((PARTS, n - 1)),
                dma((PARTS, n - 1)), dma((PARTS, n - 1)),
                dma((PARTS, n - 1)), dma((PARTS, n - 1)),
                dma((m - 1,)), dma((m - 1,)),
            ],
            compiler_params=pltpu.CompilerParams(
                collective_id=0, has_side_effects=True, vmem_limit_bytes=56 << 20
            ),
        )(user_emb.T, own, item_emb, target.reshape(1, u_dev), history.T)
        return log_rank.reshape(u_dev), metrics

    return jax.shard_map(
        body,
        mesh=mesh,
        in_specs=(P("users", "items"), P("items", None), P("users"), P("users", None)),
        out_specs=(P("users"), P()),
        check_vma=False,
    )
```

time: 73.5 us -> 69.1 us (0.940)
  local copies, waits for them, and re-layouts: 14.9 us -> 2.45 us
  Pallas kernels: 57 us -> 65.7 us
    gather x1 -> x0, local copies, waits for them, and re-layouts: 11.4 us -> none  [body(): own = item_emb[jnp.remainder(target, item_dev)]]
    pallas_call x0 -> x1, Pallas kernels: none -> 9.02 us  [body(): pl.pallas_call(pick, out_shape=jax.ShapeDtypeStruct((u_dev * 8, d), jnp.b...]
    unnamed x8 -> x2, local copies, waits for them, and re-layouts: 3.53 us -> 2.45 us
where the time goes in v2:
time: 69.1 us; the launch traced here: 68.8 us
  Pallas kernels  65.7 us (95%)
  local copies, waits for them, and re-layouts  2.45 us (4%)
    pallas_call x1, Pallas kernels, body(): pl.pallas_call(functools.partial(kernel, n, m), out_shape=(jax.ShapeDtype...  56.7 us
    pallas_call x1, Pallas kernels, body(): pl.pallas_call(pick, out_shape=jax.ShapeDtypeStruct((u_dev * 8, d), jnp.b...  9.02 us
    unnamed x2, local copies, waits for them, and re-layouts  2.45 us

profile of v2, /device:TPU:0, one launch (start us, length us, event | category | flops | bytes accessed | tf_op | source)
XLA Modules:
  0.0 68.8 jit_solution(225912547040706168)
XLA Ops:
  0.6 9.0 %shard_map.59.own_ref = bf16[8192,256]{1,0:T(8,128)(2,1)} custom-call(s32[1024]{0:T(1024)} %tgt_ref.1, bf16[32768,256]{1,0:T(8,128)(2,1)} %item_ref.3), custom_call_target="tpu_custom_call" | custom-call | tf_op jit(solution)/shard_map/pallas_call | solution.py:217
  9.7 56.7 %shard_map.60 = (f32[1,1024]{1,0:T(1,128)}, f32[2]{0:T(128)}) custom-call(bf16[32,1024]{1,0:T(8,128)(2,1)} %bitcast.5, bf16[8192,256]{1,0:T(8,128)(2,1)} %shard_map.59.own_ref, bf16[32768,256]{1,0:T(8,128)(2,1)} %item_ref.3, s32[1,1024]{1,0:T(1,128)} %bitcast.6, s32[32,1024]{1,0:T(8,128)} %bitcast.4), custom_call_target="tpu_custom_call" | custom-call | tf_op jit(solution)/shard_map/pallas_call | solution.py:224
  66.4 1.3 %copy.8 = f32[1024]{0:T(1024)} copy(f32[1024]{0:T(1024)} %bitcast.7) | data formatting | bytes 8192
  67.6 1.2 %copy.9 = f32[2]{0:T(128)} copy(f32[2]{0:T(128)} %get-tuple-element.9) | data formatting | bytes 16
